TPU v7x, 32 devices: a whole 2x2x4 slice. The times are simulated.
32 devices in a mesh: batch: 4 (over y, x), centre: 8 (over z, core).
Axes of the slice: x: 2, y: 2, z: 4, core: 2. Of those that a mesh axis runs over, the one named last changes fastest.
Arguments:
- pool: float32 [1024, 1024], P('batch', 'centre'), may hold values from -4.5 to 4.5
- sample_index: int32 [512], P('batch'), may hold values from 0 to 255
- targets: float32 [512, 256], P('batch'), may hold values from -6 to 6
- centres: float32 [512, 1024], P(('batch', 'centre')), may hold values from -4.5 to 4.5
- coeffs: float32 [512, 256], P(('batch', 'centre')), may hold values from -6 to 6
- eigvecs: float32 [512, 1024], P(('batch', 'centre')), may hold values from -0.75 to 0.75
- eigscale: float32 [1024], replicated, may hold values from 0.1 to 0.95
Outputs:
- new_coeffs: float32 [512, 256], P(('batch', 'centre'))
Inputs may be any that keep to these rules, and one draw needn't show every extreme that they name: `sample_index`: each batch row's sample lies in the block of 256 training samples held by its own batch group; the index counts within that block.
All inputs are finite; a program needn't handle non-finite values.
Results may differ from a plain program's by a relative error of at most 0.0003.
Values sent between devices are 32-bit elements; how exact they have to be, the bound alone decides.
A program may use at most 64 MiB of HBM per device.

v0:
```python
import jax
import jax.numpy as jnp
from jax import lax
from jax.experimental import pallas as pl
from jax.experimental.pallas import tpu as pltpu
from jax.sharding import PartitionSpec as P

MESH = pl.DeviceIdType.MESH
F32 = jnp.float32


def mm(a, b, dims):
    return lax.dot_general(
        a, b, (dims, ((), ())), precision=lax.Precision.HIGHEST, preferred_element_type=F32
    )


def farthest_first(z, n):
    side = z // (n // 2)
    near = z + side * (n - 1 - 2 * z)
    lone = n - 1 - 2 * near
    order = []
    for k in range(n - 1):
        paired = (k - lone + n) // n
        step = paired * (k - lone)
        beyond = near + (1 - 2 * (step % 2)) * (near - step // 2)
        chip = (1 - paired) * (n - 1 - k) + paired * beyond
        order.append(chip + side * (n - 1 - 2 * chip))
    return order


def flipped(b, k):
    bit = 1
    while bit <= k:
        if k & bit:
            b = b + bit * (1 - 2 * ((b // bit) % 2))
        bit *= 2
    return b


def rows_of(buf):
    count, depth, width = buf.shape
    if depth % 8 == 0:
        return buf[...].reshape(count * depth, width)
    return jnp.concatenate([buf[j] for j in range(count)], axis=0)


def step_kernel(
    nb, nc, inv_width, model_norm, step_size,
    pool_hbm, i_hbm, t_hbm, z_hbm, a_hbm, e_hbm, s_hbm, out_ref,
    pool_ref, i_ref, t_ref, s_ref, zcol, local, xs, ec, zs, cs, eb, pout, pin, rs, gs, gsum, cout, cin,
    x_send, x_recv, ec_send, ec_recv, b_send, b_recv,
    p_send, p_recv, r_send, r_recv, g_send, g_recv, c_send, c_recv,
):
    b = lax.axis_index("batch")
    c = lax.axis_index("centre")
    own = z_hbm.shape[0]
    part = t_hbm.shape[1]
    width = pool_hbm.shape[1]
    mate = c + 1 - 2 * lax.rem(c, 2)
    core = lax.rem(c, 2)
    half = nc // 2
    chips = farthest_first(c // 2, half)
    peers = [2 * chip + core for chip in chips]
    others = [2 * chip + side for chip in chips for side in (core, 1 - core)] + [mate]
    if nb & (nb - 1):
        groups = [lax.rem(b + k, nb) for k in range(1, nb)]
    else:
        groups = [flipped(b, k) for k in range(nb - 1, 0, -1)]
    pending = []

    def push(src, dst, send, recv, bi, ci):
        copy = pltpu.make_async_remote_copy(
            src_ref=src, dst_ref=dst, send_sem=send, recv_sem=recv,
            device_id=(bi, ci), device_id_type=MESH,
        )
        copy.start()
        pending.append(copy)

    def arrived(dst, recv):
        pltpu.make_async_remote_copy(
            src_ref=dst, dst_ref=dst, send_sem=recv, recv_sem=recv,
            device_id=(b, mate), device_id_type=MESH,
        ).wait_recv()

    barrier = pltpu.get_barrier_semaphore()
    for ci in others:
        pl.semaphore_signal(barrier, inc=1, device_id=(b, ci), device_id_type=MESH)
    for bi in groups:
        pl.semaphore_signal(barrier, inc=1, device_id=(bi, c), device_id_type=MESH)
    fetches = []
    for k, (src, dst) in enumerate([
        (pool_hbm, pool_ref), (i_hbm, i_ref), (z_hbm, zs.at[b]), (a_hbm, cs.at[b]),
        (e_hbm, ec.at[c]), (e_hbm, eb.at[b]), (s_hbm, s_ref), (t_hbm.at[c], t_ref),
    ]):
        copy = pltpu.make_async_copy(src, dst, local.at[k])
        copy.start()
        fetches.append(copy)
    fetches[0].wait()
    fetches[1].wait()
    rows = i_ref.shape[1]
    lines = lax.broadcasted_iota(jnp.int32, (pool_ref.shape[0], rows), 0)
    chosen = jnp.where(lines == i_ref[...], 1.0, 0.0).astype(F32)
    xs[c] = mm(chosen, pool_ref[...], ((0,), (0,)))
    for copy in fetches[2:]:
        copy.wait()
    pl.semaphore_wait(barrier, nc - 1 + nb - 1)

    for k, ci in enumerate(peers):
        push(xs.at[c], xs.at[c], x_send.at[k], x_recv.at[c], b, ci)
    push(xs.at[c], xs.at[c], x_send.at[half - 1], x_recv.at[c], b, mate)
    for k, bi in enumerate(groups):
        push(zs.at[b], zs.at[b], b_send.at[0, k], b_recv.at[0, b], bi, c)
    for k, bi in enumerate(groups):
        push(cs.at[b], cs.at[b], b_send.at[1, k], b_recv.at[1, b], bi, c)
    for k, ci in enumerate(peers):
        push(ec.at[c], ec.at[c], ec_send.at[k], ec_recv.at[c], b, ci)
    push(ec.at[c], ec.at[c], ec_send.at[half - 1], ec_recv.at[c], b, mate)
    for k, bi in enumerate(groups):
        push(eb.at[b], eb.at[b], b_send.at[2, k], b_recv.at[2, b], bi, c)

    for bi in groups:
        arrived(zs.at[bi], b_recv.at[0, bi])
    for j in range(nc):
        zcol[j] = zs[:, :, j * width:(j + 1) * width].reshape(nb * own, width)
    scores = mm(xs[c], zcol[c], ((1,), (1,)))
    arrived(xs.at[mate], x_recv.at[mate])
    scores = scores + mm(xs[mate], zcol[mate], ((1,), (1,)))
    for k, ci in enumerate(peers):
        arrived(xs.at[ci], x_recv.at[ci])
        push(xs.at[ci], xs.at[ci], x_send.at[half + k], x_recv.at[ci], b, mate)
        scores = scores + mm(xs[ci], zcol[ci], ((1,), (1,)))
    for ci in [2 * chip + 1 - core for chip in chips]:
        arrived(xs.at[ci], x_recv.at[ci])
        scores = scores + mm(xs[ci], zcol[ci], ((1,), (1,)))
    kernel = jnp.exp(scores * inv_width)
    for bi in groups:
        arrived(cs.at[bi], b_recv.at[1, bi])
    value = mm(kernel, rows_of(cs), ((1,), (0,)))
    for j in range(nc):
        pout[j] = value[j * part:(j + 1) * part]
    for k, ci in enumerate(others):
        push(pout.at[ci], pin.at[c], p_send.at[k], p_recv.at[c], b, ci)
    pin[c] = pout[c]

    for k, ci in enumerate(peers):
        arrived(ec.at[ci], ec_recv.at[ci])
        push(ec.at[ci], ec.at[ci], ec_send.at[half + k], ec_recv.at[ci], b, mate)

    for ci in others:
        arrived(pin.at[ci], p_recv.at[ci])
    total = pin[0]
    for j in range(1, nc):
        total = total + pin[j]
    rs[c] = total * model_norm - t_ref[...]
    for k, ci in enumerate(others):
        push(rs.at[c], rs.at[c], r_send.at[k], r_recv.at[c], b, ci)

    arrived(ec.at[mate], ec_recv.at[mate])
    for ci in [2 * chip + 1 - core for chip in chips]:
        arrived(ec.at[ci], ec_recv.at[ci])
    for bi in groups:
        arrived(eb.at[bi], b_recv.at[2, bi])
    mix = mm(rows_of(ec) * s_ref[...], rows_of(eb), ((1,), (1,)))
    kernel_t = kernel.T

    for ci in others:
        arrived(rs.at[ci], r_recv.at[ci])
    gs[b] = mm(kernel_t, rows_of(rs), ((1,), (0,)))
    for k, bi in enumerate(groups):
        push(gs.at[b], gs.at[b], g_send.at[k], g_recv.at[b], bi, c)
    for bi in groups:
        arrived(gs.at[bi], g_recv.at[bi])
    grad = gs[0]
    for j in range(1, nb):
        grad = grad + gs[j]
    grad = grad * model_norm
    gsum[...] = grad.reshape(nb, own, grad.shape[1])
    moved = mm(mix, grad, ((1,), (0,)))
    for j in range(nc):
        cout[j] = moved[j * own:(j + 1) * own]
    for k, ci in enumerate(others):
        push(cout.at[ci], cin.at[c], c_send.at[k], c_recv.at[c], b, ci)
    cin[c] = cout[c]
    for ci in others:
        arrived(cin.at[ci], c_recv.at[ci])
    fix = cin[0]
    for j in range(1, nc):
        fix = fix + cin[j]
    out_ref[...] = cs[b] - step_size * (gsum[b] - fix)
    for copy in pending:
        copy.wait_send()


def on_device(pool, sample_index, targets, centres, coeffs, eigvecs, eigscale):
    nb = lax.axis_size("batch")
    nc = lax.axis_size("centre")
    rows = sample_index.shape[0]
    part_width = pool.shape[1]
    own, features = centres.shape
    outputs = targets.shape[1]
    eigen = eigvecs.shape[1]
    total_centres = own * nb * nc
    part = rows // nc
    body = lambda *refs: step_kernel(
        nb, nc, features ** -0.5, total_centres ** -0.5,
        0.5 * (total_centres / (rows * nb)) ** 0.5, *refs
    )
    dma = pltpu.SemaphoreType.DMA
    vmem = lambda *dims: pltpu.VMEM(dims, F32)
    return pl.pallas_call(
        body,
        out_shape=jax.ShapeDtypeStruct((own, outputs), F32),
        in_specs=[pl.BlockSpec(memory_space=pltpu.HBM)] * 7,
        out_specs=pl.BlockSpec(memory_space=pltpu.VMEM),
        scratch_shapes=[
            vmem(*pool.shape),
            pltpu.VMEM((1, rows), jnp.int32),
            vmem(part, outputs),
            vmem(1, eigen),
            vmem(nc, nb * own, part_width),
            dma((8,)),
            vmem(nc, rows, part_width),
            vmem(nc, own, eigen),
            vmem(nb, own, features),
            vmem(nb, own, outputs),
            vmem(nb, own, eigen),
            vmem(nc, part, outputs),
            vmem(nc, part, outputs),
            vmem(nc, part, outputs),
            vmem(nb, nb * own, outputs),
            vmem(nb, own, outputs),
            vmem(nc, own, outputs),
            vmem(nc, own, outputs),
            dma((nc,)), dma((nc,)),
            dma((nc,)), dma((nc,)),
            dma((3, nb)), dma((3, nb)),
            dma((nc,)), dma((nc,)),
            dma((nc,)), dma((nc,)),
            dma((nb,)), dma((nb,)),
            dma((nc,)), dma((nc,)),
        ],
        compiler_params=pltpu.CompilerParams(
            collective_id=0, has_side_effects=True, vmem_limit_bytes=67043328
        ),
    )(
        pool,
        sample_index[None, :],
        targets.reshape(nc, part, outputs),
        centres,
        coeffs,
        eigvecs,
        eigscale[None, :],
    )


def solution(mesh):
    return jax.shard_map(
        on_device,
        mesh=mesh,
        in_specs=(
            P("batch", "centre"),
            P("batch"),
            P("batch", None),
            P(("batch", "centre"), None),
            P(("batch", "centre"), None),
            P(("batch", "centre"), None),
            P(),
        ),
        out_specs=P(("batch", "centre"), None),
        check_vma=False,
    )
```

profile of v0, /device:TPU:0, one launch (start us, length us, event | category | flops | bytes accessed | tf_op | source)
XLA Modules:
  0.0 37.7 jit_solution(2867204140117039960)
XLA Ops:
  0.0 36.3 %shard_map.73 = f32[16,256]{1,0:T(8,128)} custom-call(f32[256,128]{1,0:T(8,128)} %refs_0_.1, s32[1,128]{1,0:T(1,128)} %bitcast.5, f32[8,16,256]{2,1,0:T(8,128)} %bitcast.3, f32[16,1024]{1,0:T(8,128)} %refs_3_.1, f32[16,256]{1,0:T(8,128)} %refs_4_.1, f32[16,1024]{1,0:T(8,128)} %refs_5_.1, f32[1,1024]{1,0:T(1,128)} %bitcast.4), custom_call_target="tpu_custom_call" | custom-call | tf_op jit(solution)/shard_map/pallas_call | solution.py:211
  36.3 1.3 %copy.9 = f32[16,256]{1,0:T(8,128)} copy(f32[16,256]{1,0:T(8,128)} %shard_map.73) | data formatting | bytes 32768
where the time goes:
time: 37.9 us; the launch traced here: 37.7 us
  Pallas kernels  36.3 us (96%)
  local copies, waits for them, and re-layouts  1.32 us (3%)
    pallas_call x1, Pallas kernels, on_device(): pl.pallas_call(body, out_shape=jax.ShapeDtypeStruct((own, outputs), F32),...  36.3 us
    unnamed x1, local copies, waits for them, and re-layouts  1.32 us

commit v1 on v0

v1 whole, which is shorter than its diff:
```python
import jax
import jax.numpy as jnp
from jax import lax
from jax.experimental import pallas as pl
from jax.experimental.pallas import tpu as pltpu
from jax.sharding import PartitionSpec as P

MESH = pl.DeviceIdType.MESH
F32 = jnp.float32


def mm(a, b, dims):
    return lax.dot_general(
        a, b, (dims, ((), ())), precision=lax.Precision.HIGHEST, preferred_element_type=F32
    )


NN = ((1,), (0,))
NT = ((1,), (1,))


def farthest_first(z, n):
    side = z // (n // 2)
    near = z + side * (n - 1 - 2 * z)
    lone = n - 1 - 2 * near
    order = []
    for k in range(n - 1):
        paired = (k - lone + n) // n
        step = paired * (k - lone)
        beyond = near + (1 - 2 * (step % 2)) * (near - step // 2)
        chip = (1 - paired) * (n - 1 - k) + paired * beyond
        order.append(chip + side * (n - 1 - 2 * chip))
    return order


def flipped(b, k):
    bit = 1
    while bit <= k:
        if k & bit:
            b = b + bit * (1 - 2 * ((b // bit) % 2))
        bit *= 2
    return b


def flat(value):
    count, depth, width = value.shape
    if depth % 8 == 0:
        return value.reshape(count * depth, width)
    return jnp.concatenate([value[j] for j in range(count)], axis=0)


def step_kernel(
    nb, nc, inv_width, model_norm, step_size,
    pool_hbm, i_hbm, t_hbm, z_hbm, a_hbm, e_hbm, s_hbm, out_ref,
    pool_ref, i_ref, t_ref, s_ref, local,
    xg, xs, zp, zcol, ep, ej, ca, ks, mo, mt, po, fin,
    x_send, x_recv, zp_send, zp_recv, ep_send, ep_recv, ej_send, ej_recv,
    cz_send, cz_recv, cp_send, cp_recv, k_send, k_recv, m_send, m_recv, f_send, f_recv,
):
    b = lax.axis_index("batch")
    c = lax.axis_index("centre")
    nz = nc // 2
    nq = 2 * nb
    z = c // 2
    core = lax.rem(c, 2)
    mate = c + 1 - 2 * core
    own = z_hbm.shape[0]
    width = pool_hbm.shape[1]
    half = t_hbm.shape[1]
    plane = nq * own
    q = 2 * b + core
    chips = farthest_first(z, nz)
    if nb & (nb - 1):
        groups = [lax.rem(b + k, nb) for k in range(1, nb)]
    else:
        groups = [flipped(b, k) for k in range(nb - 1, 0, -1)]
    pending = []

    def push(src, dst, send, recv, bi, ci):
        copy = pltpu.make_async_remote_copy(
            src_ref=src, dst_ref=dst, send_sem=send, recv_sem=recv,
            device_id=(bi, ci), device_id_type=MESH,
        )
        copy.start()
        pending.append(copy)

    def arrived(dst, recv):
        pltpu.make_async_remote_copy(
            src_ref=dst, dst_ref=dst, send_sem=recv, recv_sem=recv,
            device_id=(b, mate), device_id_type=MESH,
        ).wait_recv()

    barrier = pltpu.get_barrier_semaphore()
    for chip in chips:
        for side in (core, 1 - core):
            pl.semaphore_signal(barrier, inc=1, device_id=(b, 2 * chip + side), device_id_type=MESH)
    for bi in groups:
        for ci in (c, mate):
            pl.semaphore_signal(barrier, inc=1, device_id=(bi, ci), device_id_type=MESH)
    pl.semaphore_signal(barrier, inc=1, device_id=(b, mate), device_id_type=MESH)
    fetches = []
    for k, (src, dst) in enumerate([
        (pool_hbm, pool_ref), (i_hbm, i_ref), (z_hbm, zp.at[q]), (e_hbm, ep.at[q]),
        (e_hbm, ej.at[z]), (a_hbm, ca.at[z, q]), (s_hbm, s_ref), (t_hbm.at[core], t_ref),
    ]):
        copy = pltpu.make_async_copy(src, dst, local.at[k])
        copy.start()
        fetches.append(copy)
    fetches[0].wait()
    fetches[1].wait()
    rows = i_ref.shape[1]
    lines = lax.broadcasted_iota(jnp.int32, (pool_ref.shape[0], rows), 0)
    chosen = jnp.where(lines == i_ref[...], 1.0, 0.0).astype(F32)
    picked = mm(chosen, pool_ref[...], ((0,), (0,)))
    for h in range(2):
        xg[h] = picked[h * half:(h + 1) * half]
    xs[c] = xg[core]
    for copy in fetches[2:]:
        copy.wait()
    pl.semaphore_wait(barrier, nc - 1 + 2 * (nb - 1))

    for k, chip in enumerate(chips):
        for j, side in enumerate((core, 1 - core)):
            push(xg.at[side], xs.at[c], x_send.at[2 * k + j], x_recv.at[c], b, 2 * chip + side)
    push(xg.at[1 - core], xs.at[c], x_send.at[nc - 2], x_recv.at[c], b, mate)
    for k, bi in enumerate(groups):
        push(zp.at[q], zp.at[q], zp_send.at[k], zp_recv.at[q], bi, c)
    push(zp.at[q], zp.at[q], zp_send.at[nb - 1], zp_recv.at[q], b, mate)
    for k, bi in enumerate(groups):
        push(ep.at[q], ep.at[q], ep_send.at[k], ep_recv.at[q], bi, c)
    push(ep.at[q], ep.at[q], ep_send.at[nb - 1], ep_recv.at[q], b, mate)
    for k, chip in enumerate(chips):
        push(ca.at[z, q], ca.at[z, q], cz_send.at[k], cz_recv.at[z], b, 2 * chip + core)
    for k, chip in enumerate(chips):
        push(ej.at[z], ej.at[z], ej_send.at[k], ej_recv.at[z], b, 2 * chip + core)

    for k, bi in enumerate(groups):
        qi = 2 * bi + core
        arrived(zp.at[qi], zp_recv.at[qi])
        push(zp.at[qi], zp.at[qi], zp_send.at[nb + k], zp_recv.at[qi], b, mate)
    arrived(zp.at[2 * b + 1 - core], zp_recv.at[2 * b + 1 - core])
    for bi in groups:
        qi = 2 * bi + 1 - core
        arrived(zp.at[qi], zp_recv.at[qi])
    for j in range(nc):
        zcol[j] = flat(zp[:, :, j * width:(j + 1) * width])
    for k, bi in enumerate(groups):
        qi = 2 * bi + core
        arrived(ep.at[qi], ep_recv.at[qi])
        push(ep.at[qi], ep.at[qi], ep_send.at[nb + k], ep_recv.at[qi], b, mate)

    scores = mm(xs[c], zcol[c], NT)
    arrived(xs.at[mate], x_recv.at[mate])
    scores = scores + mm(xs[mate], zcol[mate], NT)
    for chip in chips:
        for side in (core, 1 - core):
            ci = 2 * chip + side
            arrived(xs.at[ci], x_recv.at[ci])
            scores = scores + mm(xs[ci], zcol[ci], NT)
    kernel = jnp.exp(scores * inv_width)
    ks[z] = kernel
    for k, chip in enumerate(chips):
        push(ks.at[z], ks.at[z], k_send.at[k], k_recv.at[z], b, 2 * chip + core)

    for chip in chips:
        arrived(ca.at[chip, q], cz_recv.at[chip])
    for k, bi in enumerate(groups):
        push(ca.at[:, q], ca.at[:, q], cp_send.at[k], cp_recv.at[q], bi, c)
    push(ca.at[:, q], ca.at[:, q], cp_send.at[nb - 1], cp_recv.at[q], b, mate)

    arrived(ep.at[2 * b + 1 - core], ep_recv.at[2 * b + 1 - core])
    for bi in groups:
        qi = 2 * bi + 1 - core
        arrived(ep.at[qi], ep_recv.at[qi])
    planes = flat(ep[...])
    scale = s_ref[...]
    mo[z] = mm(ej[z] * scale, planes, NT)
    for chip in chips:
        arrived(ej.at[chip], ej_recv.at[chip])
        mo[chip] = mm(ej[chip] * scale, planes, NT)
    for k, bi in enumerate(groups):
        for j, ci in enumerate((c, mate)):
            push(mo, mt.at[:, q], m_send.at[2 * k + j], m_recv.at[q], bi, ci)
    push(mo, mt.at[:, q], m_send.at[2 * nb - 2], m_recv.at[q], b, mate)
    mt[:, q] = mo[...]

    for k, bi in enumerate(groups):
        qi = 2 * bi + core
        arrived(ca.at[:, qi], cp_recv.at[qi])
        push(ca.at[:, qi], ca.at[:, qi], cp_send.at[nb + k], cp_recv.at[qi], b, mate)
    arrived(ca.at[:, 2 * b + 1 - core], cp_recv.at[2 * b + 1 - core])
    for bi in groups:
        qi = 2 * bi + 1 - core
        arrived(ca.at[:, qi], cp_recv.at[qi])

    value = mm(kernel, flat(ca[z]), NN)
    for chip in chips:
        arrived(ks.at[chip], k_recv.at[chip])
        value = value + mm(ks[chip], flat(ca[chip]), NN)
    residual = value * model_norm - t_ref[...]

    arrived(mt.at[:, 2 * b + 1 - core], m_recv.at[2 * b + 1 - core])
    for bi in groups:
        for side in (core, 1 - core):
            qi = 2 * bi + side
            arrived(mt.at[:, qi], m_recv.at[qi])
    weights = kernel
    for j in range(nz):
        weights = weights - mm(ks[j], flat(mt[j]), NN)
    partial = mm(weights.T, residual, NN)
    for j in range(nq):
        po[j] = partial[j * own:(j + 1) * own]
    for k, bi in enumerate(groups):
        for j, side in enumerate((core, 1 - core)):
            push(po.at[2 * bi + side], fin.at[q], f_send.at[2 * k + j], f_recv.at[q], bi, 2 * z + side)
    push(po.at[2 * b + 1 - core], fin.at[q], f_send.at[2 * nb - 2], f_recv.at[q], b, mate)
    total = po[q]
    arrived(fin.at[2 * b + 1 - core], f_recv.at[2 * b + 1 - core])
    total = total + fin[2 * b + 1 - core]
    for bi in groups:
        for side in (core, 1 - core):
            qi = 2 * bi + side
            arrived(fin.at[qi], f_recv.at[qi])
            total = total + fin[qi]
    out_ref[...] = ca[z, q] - (step_size * model_norm) * total
    for copy in pending:
        copy.wait_send()


def on_device(pool, sample_index, targets, centres, coeffs, eigvecs, eigscale):
    nb = lax.axis_size("batch")
    nc = lax.axis_size("centre")
    nz = nc // 2
    nq = 2 * nb
    rows = sample_index.shape[0]
    half = rows // 2
    width = pool.shape[1]
    own, features = centres.shape
    outputs = targets.shape[1]
    eigen = eigvecs.shape[1]
    plane = own * nq
    total_centres = own * nb * nc
    body = lambda *refs: step_kernel(
        nb, nc, features ** -0.5, total_centres ** -0.5,
        0.5 * (total_centres / (rows * nb)) ** 0.5, *refs
    )
    dma = pltpu.SemaphoreType.DMA
    vmem = lambda *dims: pltpu.VMEM(dims, F32)
    return pl.pallas_call(
        body,
        out_shape=jax.ShapeDtypeStruct((own, outputs), F32),
        in_specs=[pl.BlockSpec(memory_space=pltpu.HBM)] * 7,
        out_specs=pl.BlockSpec(memory_space=pltpu.VMEM),
        scratch_shapes=[
            vmem(*pool.shape),
            pltpu.VMEM((1, rows), jnp.int32),
            vmem(half, outputs),
            vmem(1, eigen),
            dma((8,)),
            vmem(2, half, width),
            vmem(nc, half, width),
            vmem(nq, own, features),
            vmem(nc, plane, width),
            vmem(nq, own, eigen),
            vmem(nz, own, eigen),
            vmem(nz, nq, own, outputs),
            vmem(nz, half, plane),
            vmem(nz, own, plane),
            vmem(nz, nq, own, plane),
            vmem(nq, own, outputs),
            vmem(nq, own, outputs),
            dma((nc,)), dma((nc,)),
            dma((nq,)), dma((nq,)),
            dma((nq,)), dma((nq,)),
            dma((nz,)), dma((nz,)),
            dma((nz,)), dma((nz,)),
            dma((nq,)), dma((nq,)),
            dma((nz,)), dma((nz,)),
            dma((nq,)), dma((nq,)),
            dma((nq,)), dma((nq,)),
        ],
        compiler_params=pltpu.CompilerParams(
            collective_id=0, has_side_effects=True, vmem_limit_bytes=67043328
        ),
    )(
        pool,
        sample_index[None, :],
        targets.reshape(2, half, outputs),
        centres,
        coeffs,
        eigvecs,
        eigscale[None, :],
    )


def solution(mesh):
    return jax.shard_map(
        on_device,
        mesh=mesh,
        in_specs=(
            P("batch", "centre"),
            P("batch"),
            P("batch", None),
            P(("batch", "centre"), None),
            P(("batch", "centre"), None),
            P(("batch", "centre"), None),
            P(),
        ),
        out_specs=P(("batch", "centre"), None),
        check_vma=False,
    )
```

time: 37.9 us -> 33.8 us (0.89)
  Pallas kernels: 36.3 us -> 32.2 us
    pallas_call x1, Pallas kernels: 36.3 us -> 32.2 us  [on_device(): pl.pallas_call(body, out_shape=jax.ShapeDtypeStruct((own, outputs), F32),...]
where the time goes in v1:
time: 33.8 us; the launch traced here: 33.6 us
  Pallas kernels  32.2 us (95%)
  local copies, waits for them, and re-layouts  1.32 us (4%)
    pallas_call x1, Pallas kernels, on_device(): pl.pallas_call(body, out_shape=jax.ShapeDtypeStruct((own, outputs), F32),...  32.2 us
    unnamed x1, local copies, waits for them, and re-layouts  1.32 us

profile of v1, /device:TPU:0, one launch (start us, length us, event | category | flops | bytes accessed | tf_op | source)
XLA Modules:
  0.0 33.6 jit_solution(6129539516211575924)
XLA Ops:
  0.0 32.2 %shard_map.73 = f32[16,256]{1,0:T(8,128)} custom-call(f32[256,128]{1,0:T(8,128)} %refs_0_.1, s32[1,128]{1,0:T(1,128)} %bitcast.5, f32[2,64,256]{2,1,0:T(8,128)} %bitcast.3, f32[16,1024]{1,0:T(8,128)} %refs_3_.1, f32[16,256]{1,0:T(8,128)} %refs_4_.1, f32[16,1024]{1,0:T(8,128)} %refs_5_.1, f32[1,1024]{1,0:T(1,128)} %bitcast.4), custom_call_target="tpu_custom_call" | custom-call | tf_op jit(solution)/shard_map/pallas_call | solution.py:249
  32.2 1.3 %copy.9 = f32[16,256]{1,0:T(8,128)} copy(f32[16,256]{1,0:T(8,128)} %shard_map.73) | data formatting | bytes 32768

commit v2 on v1

v2 whole, which is shorter than its diff:
```python
import jax
import jax.numpy as jnp
from jax import lax
from jax.experimental import pallas as pl
from jax.experimental.pallas import tpu as pltpu
from jax.sharding import PartitionSpec as P

MESH = pl.DeviceIdType.MESH
F32 = jnp.float32
BF16 = jnp.bfloat16


def mm(a, b, dims):
    return lax.dot_general(
        a, b, (dims, ((), ())), precision=lax.Precision.HIGHEST, preferred_element_type=F32
    )


def split(value):
    high = value.astype(BF16)
    return high, (value - high.astype(F32)).astype(BF16)


def mm3(a, b, dims):
    def one(left, right):
        return lax.dot_general(left, right, (dims, ((), ())), preferred_element_type=F32)

    return one(a[0], b[0]) + (one(a[0], b[1]) + one(a[1], b[0]))


NN = ((1,), (0,))
NT = ((1,), (1,))


def farthest_first(z, n):
    side = z // (n // 2)
    near = z + side * (n - 1 - 2 * z)
    lone = n - 1 - 2 * near
    order = []
    for k in range(n - 1):
        paired = (k - lone + n) // n
        step = paired * (k - lone)
        beyond = near + (1 - 2 * (step % 2)) * (near - step // 2)
        chip = (1 - paired) * (n - 1 - k) + paired * beyond
        order.append(chip + side * (n - 1 - 2 * chip))
    return order


def flipped(b, k):
    bit = 1
    while bit <= k:
        if k & bit:
            b = b + bit * (1 - 2 * ((b // bit) % 2))
        bit *= 2
    return b


def flat(value):
    count, depth, width = value.shape
    if depth % 8 == 0:
        return value.reshape(count * depth, width)
    return jnp.concatenate([value[j] for j in range(count)], axis=0)


def step_kernel(
    nb, nc, inv_width, model_norm, step_size,
    pool_hbm, i_hbm, t_hbm, z_hbm, a_hbm, e_hbm, s_hbm, out_ref,
    pool_ref, i_ref, t_ref, s_ref, local,
    xg, xs, zp, zh, zl, ep, ej, ca, ks, mo, mt, po, fin,
    x_send, x_recv, zp_send, zp_recv, ep_send, ep_recv, ej_send, ej_recv,
    cz_send, cz_recv, cp_send, cp_recv, k_send, k_recv, m_send, m_recv, f_send, f_recv,
):
    b = lax.axis_index("batch")
    c = lax.axis_index("centre")
    nz = nc // 2
    nq = 2 * nb
    z = c // 2
    core = lax.rem(c, 2)
    mate = c + 1 - 2 * core
    own = z_hbm.shape[0]
    width = pool_hbm.shape[1]
    half = t_hbm.shape[1]
    plane = nq * own
    q = 2 * b + core
    chips = farthest_first(z, nz)
    if nb & (nb - 1):
        groups = [lax.rem(b + k, nb) for k in range(1, nb)]
    else:
        groups = [flipped(b, k) for k in range(nb - 1, 0, -1)]
    pending = []

    def push(src, dst, send, recv, bi, ci):
        copy = pltpu.make_async_remote_copy(
            src_ref=src, dst_ref=dst, send_sem=send, recv_sem=recv,
            device_id=(bi, ci), device_id_type=MESH,
        )
        copy.start()
        pending.append(copy)

    def arrived(dst, recv):
        pltpu.make_async_remote_copy(
            src_ref=dst, dst_ref=dst, send_sem=recv, recv_sem=recv,
            device_id=(b, mate), device_id_type=MESH,
        ).wait_recv()

    barrier = pltpu.get_barrier_semaphore()
    for chip in chips:
        for side in (core, 1 - core):
            pl.semaphore_signal(barrier, inc=1, device_id=(b, 2 * chip + side), device_id_type=MESH)
    for bi in groups:
        for ci in (c, mate):
            pl.semaphore_signal(barrier, inc=1, device_id=(bi, ci), device_id_type=MESH)
    pl.semaphore_signal(barrier, inc=1, device_id=(b, mate), device_id_type=MESH)
    fetches = []
    for k, (src, dst) in enumerate([
        (pool_hbm, pool_ref), (i_hbm, i_ref), (z_hbm, zp.at[q]), (e_hbm, ep.at[q]),
        (e_hbm, ej.at[z]), (a_hbm, ca.at[z, q]), (s_hbm, s_ref), (t_hbm.at[core], t_ref),
    ]):
        copy = pltpu.make_async_copy(src, dst, local.at[k])
        copy.start()
        fetches.append(copy)
    fetches[0].wait()
    fetches[1].wait()
    rows = i_ref.shape[1]
    lines = lax.broadcasted_iota(jnp.int32, (pool_ref.shape[0], rows), 0)
    chosen = jnp.where(lines == i_ref[...], 1.0, 0.0).astype(F32)
    picked = mm(chosen, pool_ref[...], ((0,), (0,)))
    for h in range(2):
        xg[h] = picked[h * half:(h + 1) * half]
    xs[c] = xg[core]
    for copy in fetches[2:]:
        copy.wait()
    pl.semaphore_wait(barrier, nc - 1 + 2 * (nb - 1))

    for k, chip in enumerate(chips):
        push(ca.at[z, q], ca.at[z, q], cz_send.at[k], cz_recv.at[z], b, 2 * chip + core)
    for k, chip in list(enumerate(chips))[:1]:
        push(ej.at[z], ej.at[z], ej_send.at[k], ej_recv.at[z], b, 2 * chip + core)
    for k, chip in enumerate(chips):
        for j, side in enumerate((core, 1 - core)):
            push(xg.at[side], xs.at[c], x_send.at[2 * k + j], x_recv.at[c], b, 2 * chip + side)
    push(xg.at[1 - core], xs.at[c], x_send.at[nc - 2], x_recv.at[c], b, mate)
    for k, chip in list(enumerate(chips))[1:]:
        push(ej.at[z], ej.at[z], ej_send.at[k], ej_recv.at[z], b, 2 * chip + core)
    for k, bi in enumerate(groups):
        push(zp.at[q], zp.at[q], zp_send.at[k], zp_recv.at[q], bi, c)
    push(zp.at[q], zp.at[q], zp_send.at[nb - 1], zp_recv.at[q], b, mate)
    for k, bi in enumerate(groups):
        push(ep.at[q], ep.at[q], ep_send.at[k], ep_recv.at[q], bi, c)
    push(ep.at[q], ep.at[q], ep_send.at[nb - 1], ep_recv.at[q], b, mate)

    twin = 2 * b + 1 - core
    near = [2 * bi + core for bi in groups]
    cross = [2 * bi + 1 - core for bi in groups]
    for chip in chips:
        arrived(ca.at[chip, q], cz_recv.at[chip])
    for k, bi in enumerate(groups):
        push(ca.at[:, q], ca.at[:, q], cp_send.at[k], cp_recv.at[q], bi, c)
    push(ca.at[:, q], ca.at[:, q], cp_send.at[nb - 1], cp_recv.at[q], b, mate)
    for k, qi in enumerate(near):
        arrived(zp.at[qi], zp_recv.at[qi])
        push(zp.at[qi], zp.at[qi], zp_send.at[nb + k], zp_recv.at[qi], b, mate)
    for qi in [twin] + cross:
        arrived(zp.at[qi], zp_recv.at[qi])
    for j in range(nc):
        zh[j], zl[j] = split(flat(zp[:, :, j * width:(j + 1) * width]))

    def score(ci):
        return mm3(split(xs[ci]), (zh[ci], zl[ci]), NT)

    scores = score(c)
    arrived(xs.at[mate], x_recv.at[mate])
    scores = scores + score(mate)
    for k, qi in enumerate(near):
        arrived(ep.at[qi], ep_recv.at[qi])
        push(ep.at[qi], ep.at[qi], ep_send.at[nb + k], ep_recv.at[qi], b, mate)
    for chip in chips:
        for side in (core, 1 - core):
            ci = 2 * chip + side
            arrived(xs.at[ci], x_recv.at[ci])
            scores = scores + score(ci)
    kernel = jnp.exp(scores * inv_width)
    ks[z] = kernel
    for k, chip in enumerate(chips):
        push(ks.at[z], ks.at[z], k_send.at[k], k_recv.at[z], b, 2 * chip + core)

    for k, qi in enumerate(near):
        arrived(ca.at[:, qi], cp_recv.at[qi])
        push(ca.at[:, qi], ca.at[:, qi], cp_send.at[nb + k], cp_recv.at[qi], b, mate)
    for qi in [twin] + cross:
        arrived(ep.at[qi], ep_recv.at[qi])
    planes = split(flat(ep[...]) * s_ref[...])
    for n, chip in enumerate([z] + chips):
        if n:
            arrived(ej.at[chip], ej_recv.at[chip])
        block = mm3(split(ej[chip]), planes, NT)
        mo[chip] = block
        for k, bi in enumerate(groups):
            for j, ci in enumerate((c, mate)):
                push(mo.at[chip], mt.at[chip, q], m_send.at[n, 2 * k + j], m_recv.at[chip, q], bi, ci)
        push(mo.at[chip], mt.at[chip, q], m_send.at[n, 2 * nb - 2], m_recv.at[chip, q], b, mate)
        mt[chip, q] = block

    for qi in [twin] + cross:
        arrived(ca.at[:, qi], cp_recv.at[qi])
    weighed = [split(kernel)]
    value = mm3(weighed[0], split(flat(ca[z])), NN)
    for chip in chips:
        coeffs = split(flat(ca[chip]))
        arrived(ks.at[chip], k_recv.at[chip])
        weighed.append(split(ks[chip]))
        value = value + mm3(weighed[-1], coeffs, NN)
    residual = split(value * model_norm - t_ref[...])

    weights = kernel
    for n, chip in enumerate([z] + chips):
        for qi in [twin] + near + cross:
            arrived(mt.at[chip, qi], m_recv.at[chip, qi])
        weights = weights - mm3(weighed[n], split(flat(mt[chip])), NN)
    partial = mm3(split(weights.T), residual, NN)
    for j in range(nq):
        po[j] = partial[j * own:(j + 1) * own]
    for k, bi in enumerate(groups):
        for j, side in enumerate((core, 1 - core)):
            push(po.at[2 * bi + side], fin.at[q], f_send.at[2 * k + j], f_recv.at[q], bi, 2 * z + side)
    push(po.at[twin], fin.at[q], f_send.at[2 * nb - 2], f_recv.at[q], b, mate)
    total = po[q]
    for qi in [twin] + near + cross:
        arrived(fin.at[qi], f_recv.at[qi])
        total = total + fin[qi]
    out_ref[...] = ca[z, q] - (step_size * model_norm) * total
    for copy in pending:
        copy.wait_send()


def on_device(pool, sample_index, targets, centres, coeffs, eigvecs, eigscale):
    nb = lax.axis_size("batch")
    nc = lax.axis_size("centre")
    nz = nc // 2
    nq = 2 * nb
    rows = sample_index.shape[0]
    half = rows // 2
    width = pool.shape[1]
    own, features = centres.shape
    outputs = targets.shape[1]
    eigen = eigvecs.shape[1]
    plane = own * nq
    total_centres = own * nb * nc
    body = lambda *refs: step_kernel(
        nb, nc, features ** -0.5, total_centres ** -0.5,
        0.5 * (total_centres / (rows * nb)) ** 0.5, *refs
    )
    dma = pltpu.SemaphoreType.DMA
    vmem = lambda *dims: pltpu.VMEM(dims, F32)
    scratch = [
        vmem(*pool.shape),
        pltpu.VMEM((1, rows), jnp.int32),
        vmem(half, outputs),
        vmem(1, eigen),
        dma((8,)),
        vmem(2, half, width),
        vmem(nc, half, width),
        vmem(nq, own, features),
        pltpu.VMEM((nc, plane, width), BF16),
        pltpu.VMEM((nc, plane, width), BF16),
        vmem(nq, own, eigen),
        vmem(nz, own, eigen),
        vmem(nz, nq, own, outputs),
        vmem(nz, half, plane),
        vmem(nz, own, plane),
        vmem(nz, nq, own, plane),
        vmem(nq, own, outputs),
        vmem(nq, own, outputs),
        dma((nc,)), dma((nc,)),
        dma((nq,)), dma((nq,)),
        dma((nq,)), dma((nq,)),
        dma((nz,)), dma((nz,)),
        dma((nz,)), dma((nz,)),
        dma((nq,)), dma((nq,)),
        dma((nz,)), dma((nz,)),
        dma((nz, nq)), dma((nz, nq)),
        dma((nq,)), dma((nq,)),
    ]
    taken = 0
    for buffer in scratch:
        if buffer.memory_space == pltpu.VMEM:
            *outer, deep, wide = buffer.shape
            size = -(-deep // 8) * 8 * (-(-wide // 128) * 128) * 4
            for extent in outer:
                size *= extent
            taken += size
    return pl.pallas_call(
        body,
        out_shape=jax.ShapeDtypeStruct((own, outputs), F32),
        in_specs=[pl.BlockSpec(memory_space=pltpu.HBM)] * 7,
        out_specs=pl.BlockSpec(memory_space=pltpu.VMEM),
        scratch_shapes=scratch,
        compiler_params=pltpu.CompilerParams(
            collective_id=0, has_side_effects=True, vmem_limit_bytes=min(taken + (12 << 20), 67043328)
        ),
    )(*[
        pltpu.with_memory_space_constraint(operand, pltpu.HBM)
        for operand in (
            pool,
            sample_index[None, :],
            targets.reshape(2, half, outputs),
            centres,
            coeffs,
            eigvecs,
            eigscale[None, :],
        )
    ])


def solution(mesh):
    return jax.shard_map(
        on_device,
        mesh=mesh,
        in_specs=(
            P("batch", "centre"),
            P("batch"),
            P("batch", None),
            P(("batch", "centre"), None),
            P(("batch", "centre"), None),
            P(("batch", "centre"), None),
            P(),
        ),
        out_specs=P(("batch", "centre"), None),
        check_vma=False,
    )
```

time: 33.8 us -> 30.6 us (0.905)
  Pallas kernels: 32.2 us -> 29.8 us
  local copies, waits for them, and re-layouts: 1.32 us -> 0.61 us
    pallas_call x1, Pallas kernels: 32.2 us -> 29.8 us  [on_device(): pl.pallas_call(body, out_shape=jax.ShapeDtypeStruct((own, outputs), F32),...]
    unnamed x1, local copies, waits for them, and re-layouts: 1.32 us -> 0.61 us
where the time goes in v2:
time: 30.6 us; the launch traced here: 30.4 us
  Pallas kernels  29.8 us (97%)
  local copies, waits for them, and re-layouts  0.61 us (2%)
    pallas_call x1, Pallas kernels, on_device(): pl.pallas_call(body, out_shape=jax.ShapeDtypeStruct((own, outputs), F32),...  29.8 us

profile of v2, /device:TPU:0, one launch (start us, length us, event | category | flops | bytes accessed | tf_op | source)
XLA Modules:
  0.0 30.4 jit_solution(17917095404127887936)
XLA Ops:
  0.0 29.8 %shard_map.73 = f32[16,256]{1,0:T(8,128)S(1)} custom-call(f32[256,128]{1,0:T(8,128)} %refs_0_.1, s32[1,128]{1,0:T(1,128)} %bitcast.5, f32[2,64,256]{2,1,0:T(8,128)} %bitcast.3, f32[16,1024]{1,0:T(8,128)} %refs_3_.1, f32[16,256]{1,0:T(8,128)} %refs_4_.1, f32[16,1024]{1,0:T(8,128)} %refs_5_.1, f32[1,1024]{1,0:T(1,128)} %bitcast.4), custom_call_target="tpu_custom_call" | custom-call | tf_op jit(solution)/shard_map/pallas_call | solution.py:292
  29.8 0.6 %copy.9 = f32[16,256]{1,0:T(8,128)} copy(f32[16,256]{1,0:T(8,128)S(1)} %shard_map.73) | data formatting | bytes 32768

commit v3 on v2

--- a/solution.py
+++ b/solution.py
@@ -25,7 +25,9 @@
     def one(left, right):
         return lax.dot_general(left, right, (dims, ((), ())), preferred_element_type=F32)
 
-    return one(a[0], b[0]) + (one(a[0], b[1]) + one(a[1], b[0]))
+    rows = a[0].shape[0]
+    both = one(jnp.concatenate(a, axis=0), b[0])
+    return both[:rows] + (both[rows:] + one(a[0], b[1]))
 
 
 NN = ((1,), (0,))
@@ -66,8 +68,8 @@
     nb, nc, inv_width, model_norm, step_size,
     pool_hbm, i_hbm, t_hbm, z_hbm, a_hbm, e_hbm, s_hbm, out_ref,
     pool_ref, i_ref, t_ref, s_ref, local,
-    xg, xs, zp, zh, zl, ep, ej, ca, ks, mo, mt, po, fin,
-    x_send, x_recv, zp_send, zp_recv, ep_send, ep_recv, ej_send, ej_recv,
+    xg, xs, zp, zh, zl, ep, eq, ej, ca, ks, me, mo, mt, po, fin,
+    x_send, x_recv, zp_send, zp_recv, ep_send, ep_recv, eq_send, eq_recv, ej_send, ej_recv,
     cz_send, cz_recv, cp_send, cp_recv, k_send, k_recv, m_send, m_recv, f_send, f_recv,
 ):
     b = lax.axis_index("batch")
@@ -83,6 +85,9 @@
     plane = nq * own
     q = 2 * b + core
     chips = farthest_first(z, nz)
+    rank, parity = z // 2, lax.rem(z, 2)
+    sib = z + 1 - 2 * parity
+    kin = farthest_first(rank, nz // 2)
     if nb & (nb - 1):
         groups = [lax.rem(b + k, nb) for k in range(1, nb)]
     else:
@@ -108,13 +113,13 @@
         for side in (core, 1 - core):
             pl.semaphore_signal(barrier, inc=1, device_id=(b, 2 * chip + side), device_id_type=MESH)
     for bi in groups:
-        for ci in (c, mate):
+        for ci in (c, mate, 2 * sib, 2 * sib + 1):
             pl.semaphore_signal(barrier, inc=1, device_id=(bi, ci), device_id_type=MESH)
     pl.semaphore_signal(barrier, inc=1, device_id=(b, mate), device_id_type=MESH)
     fetches = []
     for k, (src, dst) in enumerate([
         (pool_hbm, pool_ref), (i_hbm, i_ref), (z_hbm, zp.at[q]), (e_hbm, ep.at[q]),
-        (e_hbm, ej.at[z]), (a_hbm, ca.at[z, q]), (s_hbm, s_ref), (t_hbm.at[core], t_ref),
+        (a_hbm, ca.at[z, q]), (s_hbm, s_ref), (t_hbm.at[core], t_ref),
     ]):
         copy = pltpu.make_async_copy(src, dst, local.at[k])
         copy.start()
@@ -130,18 +135,17 @@
     xs[c] = xg[core]
     for copy in fetches[2:]:
         copy.wait()
-    pl.semaphore_wait(barrier, nc - 1 + 2 * (nb - 1))
+    pl.semaphore_wait(barrier, nc - 1 + 4 * (nb - 1))
 
     for k, chip in enumerate(chips):
         push(ca.at[z, q], ca.at[z, q], cz_send.at[k], cz_recv.at[z], b, 2 * chip + core)
-    for k, chip in list(enumerate(chips))[:1]:
-        push(ej.at[z], ej.at[z], ej_send.at[k], ej_recv.at[z], b, 2 * chip + core)
+    push(ep.at[q], eq.at[q], eq_send.at[nq], eq_recv.at[q], b, 2 * sib + core)
     for k, chip in enumerate(chips):
         for j, side in enumerate((core, 1 - core)):
             push(xg.at[side], xs.at[c], x_send.at[2 * k + j], x_recv.at[c], b, 2 * chip + side)
     push(xg.at[1 - core], xs.at[c], x_send.at[nc - 2], x_recv.at[c], b, mate)
-    for k, chip in list(enumerate(chips))[1:]:
-        push(ej.at[z], ej.at[z], ej_send.at[k], ej_recv.at[z], b, 2 * chip + core)
+    for k, other in enumerate(kin):
+        push(ep.at[q], ej.at[rank], ej_send.at[k], ej_recv.at[rank], b, 2 * (2 * other + parity) + core)
     for k, bi in enumerate(groups):
         push(zp.at[q], zp.at[q], zp_send.at[k], zp_recv.at[q], bi, c)
     push(zp.at[q], zp.at[q], zp_send.at[nb - 1], zp_recv.at[q], b, mate)
@@ -152,6 +156,10 @@
     twin = 2 * b + 1 - core
     near = [2 * bi + core for bi in groups]
     cross = [2 * bi + 1 - core for bi in groups]
+    arrived(eq.at[q], eq_recv.at[q])
+    for k, bi in enumerate(groups):
+        push(eq.at[q], eq.at[q], eq_send.at[k], eq_recv.at[q], bi, c)
+    push(eq.at[q], eq.at[q], eq_send.at[nb - 1], eq_recv.at[q], b, mate)
     for chip in chips:
         arrived(ca.at[chip, q], cz_recv.at[chip])
     for k, bi in enumerate(groups):
@@ -184,39 +192,65 @@
     for k, chip in enumerate(chips):
         push(ks.at[z], ks.at[z], k_send.at[k], k_recv.at[z], b, 2 * chip + core)
 
+    for qi in [twin] + cross:
+        arrived(ep.at[qi], ep_recv.at[qi])
+    planes = split(flat(ep[...]) * s_ref[...])
+    me[parity] = mm3(split(ep[q]), planes, NT)
+    me[1 - parity] = mm3(split(eq[q]), planes, NT)
+    for k, bi in enumerate(groups):
+        for j, ci in enumerate((c, mate)):
+            push(me, mt.at[rank, :, q], m_send.at[0, 2 * k + j], m_recv.at[rank, parity, q], bi, ci)
+    push(me, mt.at[rank, :, q], m_send.at[0, nq - 2], m_recv.at[rank, parity, q], b, mate)
+    mt[rank, :, q] = me[...]
+    for k, qi in enumerate(near):
+        arrived(eq.at[qi], eq_recv.at[qi])
+        push(eq.at[qi], eq.at[qi], eq_send.at[nb + k], eq_recv.at[qi], b, mate)
+    for n, other in enumerate(kin):
+        arrived(ej.at[other], ej_recv.at[other])
+        lines = split(ej[other])
+        here = mt.at[other, parity, q]
+        mo[n, 0] = mm3(lines, planes, NT)
+        for k, bi in enumerate(groups):
+            for j, ci in enumerate((c, mate)):
+                push(mo.at[n, 0], here, m_send.at[n + 1, 2 * k + j], m_recv.at[other, parity, q], bi, ci)
+        push(mo.at[n, 0], here, m_send.at[n + 1, nq - 2], m_recv.at[other, parity, q], b, mate)
+        mt[other, parity, q] = mo[n, 0]
+    for qi in [twin] + cross:
+        arrived(eq.at[qi], eq_recv.at[qi])
+    sibs = split(flat(eq[...]) * s_ref[...])
+    for n, other in enumerate(kin):
+        lines = split(ej[other])
+        here = mt.at[other, parity, q]
+        mo[n, 1] = mm3(lines, sibs, NT)
+        for k, bi in enumerate(groups):
+            for side in range(2):
+                push(mo.at[n, 1], here, m_send.at[n + 1, nq + 2 * k + side], m_recv.at[other, parity, q], bi, 2 * sib + side)
+        for side in range(2):
+            push(mo.at[n, 1], here, m_send.at[n + 1, 2 * nq - 2 + side], m_recv.at[other, parity, q], b, 2 * sib + side)
+
     for k, qi in enumerate(near):
         arrived(ca.at[:, qi], cp_recv.at[qi])
         push(ca.at[:, qi], ca.at[:, qi], cp_send.at[nb + k], cp_recv.at[qi], b, mate)
     for qi in [twin] + cross:
-        arrived(ep.at[qi], ep_recv.at[qi])
-    planes = split(flat(ep[...]) * s_ref[...])
-    for n, chip in enumerate([z] + chips):
-        if n:
-            arrived(ej.at[chip], ej_recv.at[chip])
-        block = mm3(split(ej[chip]), planes, NT)
-        mo[chip] = block
-        for k, bi in enumerate(groups):
-            for j, ci in enumerate((c, mate)):
-                push(mo.at[chip], mt.at[chip, q], m_send.at[n, 2 * k + j], m_recv.at[chip, q], bi, ci)
-        push(mo.at[chip], mt.at[chip, q], m_send.at[n, 2 * nb - 2], m_recv.at[chip, q], b, mate)
-        mt[chip, q] = block
-
-    for qi in [twin] + cross:
         arrived(ca.at[:, qi], cp_recv.at[qi])
-    weighed = [split(kernel)]
-    value = mm3(weighed[0], split(flat(ca[z])), NN)
+    value = mm3(split(kernel), split(flat(ca[z])), NN)
     for chip in chips:
         coeffs = split(flat(ca[chip]))
         arrived(ks.at[chip], k_recv.at[chip])
-        weighed.append(split(ks[chip]))
-        value = value + mm3(weighed[-1], coeffs, NN)
+        value = value + mm3(split(ks[chip]), coeffs, NN)
     residual = split(value * model_norm - t_ref[...])
 
     weights = kernel
-    for n, chip in enumerate([z] + chips):
-        for qi in [twin] + near + cross:
-            arrived(mt.at[chip, qi], m_recv.at[chip, qi])
-        weights = weights - mm3(weighed[n], split(flat(mt[chip])), NN)
+    for qi in [twin] + near + cross:
+        arrived(mt.at[rank, :, qi], m_recv.at[rank, parity, qi])
+    for n, other in enumerate([rank] + kin):
+        if n:
+            for qi in [twin] + near + cross:
+                arrived(mt.at[other, parity, qi], m_recv.at[other, parity, qi])
+            for qi in [q, twin] + near + cross:
+                arrived(mt.at[other, 1 - parity, qi], m_recv.at[other, 1 - parity, qi])
+        for side in range(2):
+            weights = weights - mm3(split(ks[2 * other + side]), split(flat(mt[other, side])), NN)
     partial = mm3(split(weights.T), residual, NN)
     for j in range(nq):
         po[j] = partial[j * own:(j + 1) * own]
@@ -264,21 +298,24 @@
         pltpu.VMEM((nc, plane, width), BF16),
         pltpu.VMEM((nc, plane, width), BF16),
         vmem(nq, own, eigen),
-        vmem(nz, own, eigen),
+        vmem(nq, own, eigen),
+        vmem(nz // 2, own, eigen),
         vmem(nz, nq, own, outputs),
         vmem(nz, half, plane),
-        vmem(nz, own, plane),
-        vmem(nz, nq, own, plane),
+        vmem(2, own, plane),
+        vmem(nz // 2 - 1, 2, own, plane),
+        vmem(nz // 2, 2, nq, own, plane),
         vmem(nq, own, outputs),
         vmem(nq, own, outputs),
         dma((nc,)), dma((nc,)),
         dma((nq,)), dma((nq,)),
         dma((nq,)), dma((nq,)),
+        dma((nq + 1,)), dma((nq,)),
         dma((nz,)), dma((nz,)),
         dma((nz,)), dma((nz,)),
         dma((nq,)), dma((nq,)),
         dma((nz,)), dma((nz,)),
-        dma((nz, nq)), dma((nz, nq)),
+        dma((nz // 2, 2 * nq)), dma((nz // 2, 2, nq)),
         dma((nq,)), dma((nq,)),
     ]
     taken = 0

time: 30.6 us -> 29.9 us (0.977)
  Pallas kernels: 29.8 us -> 29.2 us
    pallas_call x1, Pallas kernels: 29.8 us -> 29.2 us  [on_device(): pl.pallas_call(body, out_shape=jax.ShapeDtypeStruct((own, outputs), F32),...]
where the time goes in v3:
time: 29.9 us; the launch traced here: 29.8 us
  Pallas kernels  29.2 us (98%)
  local copies, waits for them, and re-layouts  0.61 us (2%)
    pallas_call x1, Pallas kernels, on_device(): pl.pallas_call(body, out_shape=jax.ShapeDtypeStruct((own, outputs), F32),...  29.2 us
    unnamed x1, local copies, waits for them, and re-layouts  0.61 us

profile of v3, /device:TPU:0, one launch (start us, length us, event | category | flops | bytes accessed | tf_op | source)
XLA Modules:
  0.0 29.8 jit_solution(10603500935493933921)
XLA Ops:
  0.0 29.2 %shard_map.73 = f32[16,256]{1,0:T(8,128)S(1)} custom-call(f32[256,128]{1,0:T(8,128)} %refs_0_.1, s32[1,128]{1,0:T(1,128)} %bitcast.5, f32[2,64,256]{2,1,0:T(8,128)} %bitcast.3, f32[16,1024]{1,0:T(8,128)} %refs_3_.1, f32[16,256]{1,0:T(8,128)} %refs_4_.1, f32[16,1024]{1,0:T(8,128)} %refs_5_.1, f32[1,1024]{1,0:T(1,128)} %bitcast.4), custom_call_target="tpu_custom_call" | custom-call | tf_op jit(solution)/shard_map/pallas_call | solution.py:329
  29.2 0.6 %copy.9 = f32[16,256]{1,0:T(8,128)} copy(f32[16,256]{1,0:T(8,128)S(1)} %shard_map.73) | data formatting | bytes 32768

commit v4 on v3

--- a/solution.py
+++ b/solution.py
@@ -157,7 +157,7 @@
     near = [2 * bi + core for bi in groups]
     cross = [2 * bi + 1 - core for bi in groups]
     arrived(eq.at[q], eq_recv.at[q])
-    for k, bi in enumerate(groups):
+    for k, bi in list(enumerate(groups))[1:]:
         push(eq.at[q], eq.at[q], eq_send.at[k], eq_recv.at[q], bi, c)
     push(eq.at[q], eq.at[q], eq_send.at[nb - 1], eq_recv.at[q], b, mate)
     for chip in chips:
@@ -182,6 +182,8 @@
     for k, qi in enumerate(near):
         arrived(ep.at[qi], ep_recv.at[qi])
         push(ep.at[qi], ep.at[qi], ep_send.at[nb + k], ep_recv.at[qi], b, mate)
+        if k == 0:
+            push(ep.at[qi], eq.at[qi], eq_send.at[0], eq_recv.at[qi], b, 2 * sib + core)
     for chip in chips:
         for side in (core, 1 - core):
             ci = 2 * chip + side
@@ -198,9 +200,8 @@
     me[parity] = mm3(split(ep[q]), planes, NT)
     me[1 - parity] = mm3(split(eq[q]), planes, NT)
     for k, bi in enumerate(groups):
-        for j, ci in enumerate((c, mate)):
-            push(me, mt.at[rank, :, q], m_send.at[0, 2 * k + j], m_recv.at[rank, parity, q], bi, ci)
-    push(me, mt.at[rank, :, q], m_send.at[0, nq - 2], m_recv.at[rank, parity, q], b, mate)
+        push(me, mt.at[rank, :, q], m_send.at[0, k], m_recv.at[rank, parity, q], bi, c)
+    push(me, mt.at[rank, :, q], m_send.at[0, nb - 1], m_recv.at[rank, parity, q], b, mate)
     mt[rank, :, q] = me[...]
     for k, qi in enumerate(near):
         arrived(eq.at[qi], eq_recv.at[qi])
@@ -233,6 +234,9 @@
         push(ca.at[:, qi], ca.at[:, qi], cp_send.at[nb + k], cp_recv.at[qi], b, mate)
     for qi in [twin] + cross:
         arrived(ca.at[:, qi], cp_recv.at[qi])
+    for k, qi in enumerate(near):
+        arrived(mt.at[rank, :, qi], m_recv.at[rank, parity, qi])
+        push(mt.at[rank, :, qi], mt.at[rank, :, qi], m_send.at[0, nb + k], m_recv.at[rank, parity, qi], b, mate)
     value = mm3(split(kernel), split(flat(ca[z])), NN)
     for chip in chips:
         coeffs = split(flat(ca[chip]))
@@ -241,7 +245,7 @@
     residual = split(value * model_norm - t_ref[...])
 
     weights = kernel
-    for qi in [twin] + near + cross:
+    for qi in [twin] + cross:
         arrived(mt.at[rank, :, qi], m_recv.at[rank, parity, qi])
     for n, other in enumerate([rank] + kin):
         if n:
@@ -252,6 +256,7 @@
         for side in range(2):
             weights = weights - mm3(split(ks[2 * other + side]), split(flat(mt[other, side])), NN)
     partial = mm3(split(weights.T), residual, NN)
+    last = nq - 1
     for j in range(nq):
         po[j] = partial[j * own:(j + 1) * own]
     for k, bi in enumerate(groups):
@@ -259,11 +264,13 @@
             push(po.at[2 * bi + side], fin.at[q], f_send.at[2 * k + j], f_recv.at[q], bi, 2 * z + side)
     push(po.at[twin], fin.at[q], f_send.at[2 * nb - 2], f_recv.at[q], b, mate)
     total = po[q]
+    for copy in pending[:-last]:
+        copy.wait_send()
     for qi in [twin] + near + cross:
         arrived(fin.at[qi], f_recv.at[qi])
         total = total + fin[qi]
     out_ref[...] = ca[z, q] - (step_size * model_norm) * total
-    for copy in pending:
+    for copy in pending[-last:]:
         copy.wait_send()
 
 

time: 29.9 us -> 29.5 us (0.987)
  Pallas kernels: 29.2 us -> 28.8 us
    pallas_call x1, Pallas kernels: 29.2 us -> 28.8 us  [on_device(): pl.pallas_call(body, out_shape=jax.ShapeDtypeStruct((own, outputs), F32),...]
where the time goes in v4:
time: 29.5 us; the launch traced here: 29.4 us
  Pallas kernels  28.8 us (98%)
  local copies, waits for them, and re-layouts  0.61 us (2%)
    pallas_call x1, Pallas kernels, on_device(): pl.pallas_call(body, out_shape=jax.ShapeDtypeStruct((own, outputs), F32),...  28.8 us
    unnamed x1, local copies, waits for them, and re-layouts  0.61 us

profile of v4, /device:TPU:0, one launch (start us, length us, event | category | flops | bytes accessed | tf_op | source)
XLA Modules:
  0.0 29.4 jit_solution(8303046897595975128)
XLA Ops:
  0.0 28.8 %shard_map.73 = f32[16,256]{1,0:T(8,128)S(1)} custom-call(f32[256,128]{1,0:T(8,128)} %refs_0_.1, s32[1,128]{1,0:T(1,128)} %bitcast.5, f32[2,64,256]{2,1,0:T(8,128)} %bitcast.3, f32[16,1024]{1,0:T(8,128)} %refs_3_.1, f32[16,256]{1,0:T(8,128)} %refs_4_.1, f32[16,1024]{1,0:T(8,128)} %refs_5_.1, f32[1,1024]{1,0:T(1,128)} %bitcast.4), custom_call_target="tpu_custom_call" | custom-call | tf_op jit(solution)/shard_map/pallas_call | solution.py:336
  28.8 0.6 %copy.9 = f32[16,256]{1,0:T(8,128)} copy(f32[16,256]{1,0:T(8,128)S(1)} %shard_map.73) | data formatting | bytes 32768

commit v5 on v4

--- a/solution.py
+++ b/solution.py
@@ -68,7 +68,7 @@
     nb, nc, inv_width, model_norm, step_size,
     pool_hbm, i_hbm, t_hbm, z_hbm, a_hbm, e_hbm, s_hbm, out_ref,
     pool_ref, i_ref, t_ref, s_ref, local,
-    xg, xs, zp, zh, zl, ep, eq, ej, ca, ks, me, mo, mt, po, fin,
+    xg, xs, zp, zh, zl, ep, eq, ej, ca, ks, gh, gl, me, mo, mt, po, fin,
     x_send, x_recv, zp_send, zp_recv, ep_send, ep_recv, eq_send, eq_recv, ej_send, ej_recv,
     cz_send, cz_recv, cp_send, cp_recv, k_send, k_recv, m_send, m_recv, f_send, f_recv,
 ):
@@ -244,7 +244,9 @@
         value = value + mm3(split(ks[chip]), coeffs, NN)
     residual = split(value * model_norm - t_ref[...])
 
-    weights = kernel
+    for j in range(nz):
+        gh[j], gl[j] = split(mm3(split(ks[j].T), residual, NN))
+    partial = mm3(split(kernel.T), residual, NN)
     for qi in [twin] + cross:
         arrived(mt.at[rank, :, qi], m_recv.at[rank, parity, qi])
     for n, other in enumerate([rank] + kin):
@@ -254,8 +256,8 @@
             for qi in [q, twin] + near + cross:
                 arrived(mt.at[other, 1 - parity, qi], m_recv.at[other, 1 - parity, qi])
         for side in range(2):
-            weights = weights - mm3(split(ks[2 * other + side]), split(flat(mt[other, side])), NN)
-    partial = mm3(split(weights.T), residual, NN)
+            field = (gh[2 * other + side], gl[2 * other + side])
+            partial = partial - mm3(split(flat(mt[other, side]).T), field, NN)
     last = nq - 1
     for j in range(nq):
         po[j] = partial[j * own:(j + 1) * own]
@@ -309,6 +311,8 @@
         vmem(nz // 2, own, eigen),
         vmem(nz, nq, own, outputs),
         vmem(nz, half, plane),
+        pltpu.VMEM((nz, plane, outputs), BF16),
+        pltpu.VMEM((nz, plane, outputs), BF16),
         vmem(2, own, plane),
         vmem(nz // 2 - 1, 2, own, plane),
         vmem(nz // 2, 2, nq, own, plane),

time: 29.5 us -> 29.4 us (level)
  no operation moved by 1% of the time
where the time goes in v5:
time: 29.4 us; the launch traced here: 29.2 us
  Pallas kernels  28.6 us (97%)
  local copies, waits for them, and re-layouts  0.61 us (2%)
    pallas_call x1, Pallas kernels, on_device(): pl.pallas_call(body, out_shape=jax.ShapeDtypeStruct((own, outputs), F32),...  28.6 us
    unnamed x1, local copies, waits for them, and re-layouts  0.61 us

profile of v5, /device:TPU:0, one launch (start us, length us, event | category | flops | bytes accessed | tf_op | source)
XLA Modules:
  0.0 29.2 jit_solution(1827001671280777052)
XLA Ops:
  0.0 28.6 %shard_map.73 = f32[16,256]{1,0:T(8,128)S(1)} custom-call(f32[256,128]{1,0:T(8,128)} %refs_0_.1, s32[1,128]{1,0:T(1,128)} %bitcast.5, f32[2,64,256]{2,1,0:T(8,128)} %bitcast.3, f32[16,1024]{1,0:T(8,128)} %refs_3_.1, f32[16,256]{1,0:T(8,128)} %refs_4_.1, f32[16,1024]{1,0:T(8,128)} %refs_5_.1, f32[1,1024]{1,0:T(1,128)} %bitcast.4), custom_call_target="tpu_custom_call" | custom-call | tf_op jit(solution)/shard_map/pallas_call | solution.py:340
  28.6 0.6 %copy.9 = f32[16,256]{1,0:T(8,128)} copy(f32[16,256]{1,0:T(8,128)S(1)} %shard_map.73) | data formatting | bytes 32768
